TPU v7x, 256 devices: a whole 4x4x8 slice. The times are simulated.
256 devices in a mesh: cp: 32 (over y_lo, z, core), tp: 8 (over x, y_hi).
Axes of the slice: x: 4, y: 4 (y_hi: 2, y_lo: 2; y = y_hi * 2 + y_lo), z: 8, core: 2. Of those that a mesh axis runs over, the one named last changes fastest.
Arguments:
- hidden_in: bfloat16 [8192, 5120], P('cp', 'tp'), may hold values from -6 to 6
- norm_gain: float32 [5120], replicated, may hold values from 0.25 to 1.75
- seq_lengths: int32 [16], replicated, may hold values from 1 to 6144, 8192 in all
- w_query: bfloat16 [5120, 3072], P(None, 'tp'), may hold values from -0.078125 to 0.078125
- b_query: bfloat16 [3072], P('tp'), may hold values from -400 to 400
- w_key: bfloat16 [5120, 1024], P(None, 'tp'), may hold values from -0.078125 to 0.078125
- b_key: bfloat16 [1024], P('tp'), may hold values from -3 to 3
- w_value: bfloat16 [5120, 1024], P(None, 'tp'), may hold values from -0.078125 to 0.078125
- b_value: bfloat16 [1024], P('tp'), may hold values from -3 to 3
- w_out: bfloat16 [3072, 5120], P(None, 'tp'), may hold values from -0.109375 to 0.109375
Outputs:
- mixed: bfloat16 [8192, 5120], P('cp', 'tp')
- k_cache: bfloat16 [8192, 1024], P('cp', 'tp')
- v_cache: bfloat16 [8192, 1024], P('cp', 'tp')
Inputs may be any that keep to these rules, and one draw needn't show every extreme that they name: `seq_lengths`: they sum to 8192; the longest is exactly 6144.
All inputs are finite; a program needn't handle non-finite values.
Results may differ from a plain program's by a relative error of at most 0.012.
The roundings to bfloat16 on the way count: a program that leaves them out, or rounds other values in their place, can miss the bound.
Values may be sent and summed in bfloat16 or wider, within the bound.
A program may use at most 64 MiB of HBM per device.

v0:
```python
import functools

import jax
import jax.numpy as jnp
from jax import lax
from jax.experimental import pallas as pl
from jax.experimental.pallas import tpu as pltpu
from jax.sharding import PartitionSpec as P

HD = 128
EPS = 1e-06
ROPE_BASE = 1000000.0
NEG = -1e30
MESH = pl.DeviceIdType.MESH
BF = jnp.bfloat16
F32 = jnp.float32
LEFT, RIGHT, OPP, PART, PLEFT, PRIGHT, POPP = 1, 2, 3, 4, 5, 6, 7
SENDS = 80


def kernel(
    hid, gain, seq, wq, bq, wk, bk, wv, bv, wo, freq,
    mixed, kout, vout,
    G, N, W, Wo, Kb, Vb, AT, Q, M, L, ACC, COS, SIN, START, SS, OACC,
    lsem, a_send, a_recv, c_send, c_recv, kv_send, kv_recv,
):
    T = hid.shape[0]
    D1 = hid.shape[1]
    H1 = wo.shape[0] // 8
    NH = H1 // HD
    half = T // 2
    cp = lax.axis_index("cp")
    tp = lax.axis_index("tp")
    y = lax.div(cp, 16)
    z = lax.div(lax.rem(cp, 16), 2)
    k = lax.rem(cp, 2)
    x = lax.div(tp, 2)
    yh = lax.rem(tp, 2)
    xl = lax.rem(x + 3, 4)
    xr = lax.rem(x + 1, 4)
    xo = lax.rem(x + 2, 4)
    right = (cp, 2 * xr + yh)
    left = (cp, 2 * xl + yh)
    partner = (cp, 2 * x + 1 - yh)
    zplus = (y * 16 + lax.rem(z + 1, 8) * 2 + k, tp)
    zminus = (y * 16 + lax.rem(z + 7, 8) * 2 + k, tp)
    ypart = ((1 - y) * 16 + z * 2 + k, tp)
    sib = (y * 16 + z * 2 + 1 - k, tp)

    own_cols = pl.ds(pl.multiple_of(tp * D1, 128), D1)
    load_hid = pltpu.make_async_copy(hid, G.at[:, own_cols], lsem.at[0])
    load_hid.start()
    loads = [
        pltpu.make_async_copy(wk, W.at[:, pl.ds(H1, HD)], lsem.at[1]),
        pltpu.make_async_copy(wv, W.at[:, pl.ds(H1 + HD, HD)], lsem.at[2]),
        pltpu.make_async_copy(wq, W.at[:, pl.ds(0, H1)], lsem.at[3]),
        pltpu.make_async_copy(wo, Wo, lsem.at[4]),
    ]

    barrier = pltpu.get_barrier_semaphore()
    for dev in (right, left, partner, zplus, zminus, ypart, sib):
        pl.semaphore_signal(barrier, inc=1, device_id=dev, device_id_type=MESH)
    for c in loads:
        c.start()
    pl.semaphore_wait(barrier, 7)
    load_hid.wait()

    tps = {
        0: 2 * x + yh, LEFT: 2 * xl + yh, RIGHT: 2 * xr + yh, OPP: 2 * xo + yh,
        PART: 2 * x + 1 - yh, PLEFT: 2 * xl + 1 - yh, PRIGHT: 2 * xr + 1 - yh, POPP: 2 * xo + 1 - yh,
    }

    class Gather:
        def __init__(self, buf, width, ssem, rsem):
            self.buf, self.width, self.ssem, self.rsem = buf, width, ssem, rsem
            self.sent = []

        def ref(self, slot, h):
            cols = pl.ds(pl.multiple_of(tps[slot] * self.width, 128), self.width)
            return self.buf.at[pl.ds(h * half, half), cols]

        def send(self, slot, h, dev, dst_slot):
            r = self.ref(slot, h)
            c = pltpu.make_async_remote_copy(
                src_ref=r, dst_ref=r, send_sem=self.ssem.at[len(self.sent)],
                recv_sem=self.rsem.at[dst_slot * 2 + h], device_id=dev, device_id_type=MESH,
            )
            c.start()
            self.sent.append(c)

        def wait(self, slot, h):
            r = self.ref(slot, h)
            pltpu.make_async_remote_copy(
                src_ref=r, dst_ref=r, send_sem=self.ssem.at[0],
                recv_sem=self.rsem.at[slot * 2 + h], device_id=right, device_id_type=MESH,
            ).wait_recv()

        def start(self):
            self.send(0, 0, right, LEFT)
            self.send(0, 1, left, RIGHT)
            self.send(0, 0, partner, PART)
            self.send(0, 1, right, LEFT)
            self.send(0, 0, left, RIGHT)
            self.send(0, 1, partner, PART)

        def run(self, hooks):
            self.wait(LEFT, 0)
            self.send(LEFT, 0, right, OPP)
            self.wait(RIGHT, 1)
            self.send(RIGHT, 1, left, OPP)
            hooks[0]()
            self.wait(PART, 0)
            self.send(PART, 0, right, PLEFT)
            self.send(PART, 0, left, PRIGHT)
            self.wait(PART, 1)
            self.send(PART, 1, left, PRIGHT)
            self.send(PART, 1, right, PLEFT)
            self.wait(LEFT, 1)
            self.wait(RIGHT, 0)
            hooks[1]()
            self.wait(PLEFT, 0)
            self.send(PLEFT, 0, right, POPP)
            self.wait(PRIGHT, 1)
            self.send(PRIGHT, 1, left, POPP)
            self.wait(OPP, 0)
            self.wait(OPP, 1)
            hooks[2]()
            self.wait(PLEFT, 1)
            self.wait(PRIGHT, 0)
            hooks[3]()
            self.wait(POPP, 0)
            self.wait(POPP, 1)
            hooks[4]()

        def drain(self):
            for c in self.sent:
                c.wait_send()

    ga = Gather(G, D1, a_send, a_recv)
    ga.start()

    tok = lax.broadcasted_iota(jnp.int32, (T, HD), 0) + cp * T
    first = jnp.zeros((T, HD), jnp.int32)
    run_start = jnp.int32(0)
    for j in range(seq.shape[0]):
        first = jnp.where(tok >= run_start, run_start, first)
        run_start = run_start + seq[j]
    START[...] = first
    angle = (tok - first).astype(F32) * freq[...]
    COS[...] = jnp.cos(angle)
    sgn = jnp.where(lax.broadcasted_iota(jnp.int32, (T, HD), 1) < HD // 2, -1.0, 1.0)
    SIN[...] = jnp.sin(angle) * sgn

    def slab(slot):
        return pl.ds(pl.multiple_of(tps[slot] * D1, 128), D1)

    def squares(slots, init=False):
        total = None if init else SS[...]
        for s in slots:
            v = G[:, slab(s)].astype(F32)
            v = v * v
            for c in range(D1 // HD):
                piece = v[:, c * HD:(c + 1) * HD]
                total = piece if total is None else total + piece
        SS[...] = total

    ga.run([
        lambda: squares((0,), True),
        lambda: squares((LEFT, RIGHT, PART)),
        lambda: squares((OPP,)),
        lambda: squares((PLEFT, PRIGHT)),
        lambda: squares((POPP,)),
    ])
    loads[0].wait()
    loads[1].wait()
    inv = lax.rsqrt(jnp.sum(SS[...], axis=1, keepdims=True) / (8.0 * D1) + EPS)
    pair = 2 * D1
    kv = None
    for i in range(4):
        sl = slice(i * pair, (i + 1) * pair)
        n = (G[:, sl].astype(F32) * inv * gain[:, sl]).astype(BF)
        N[:, sl] = n
        part = jnp.dot(n, W[sl, H1:], preferred_element_type=F32)
        kv = part if kv is None else kv + part

    def rope(u):
        return u * COS[...] + pltpu.roll(u, HD // 2, 1) * SIN[...]

    mine = cp
    knew = rope(kv[:, :HD] + bk[...].astype(F32)).astype(BF)
    vnew = (kv[:, HD:] + bv[...].astype(F32)).astype(BF)
    Kb[mine] = knew
    Vb[mine] = vnew
    kout[...] = knew
    vout[...] = vnew

    sent = []

    def piece(part, p, s, kk):
        blk = p * 16 + s * 2 + kk
        return (Kb if part == 0 else Vb).at[blk], kv_recv.at[part * 32 + blk]

    def send(cond, part, p, s, dev):
        r, rs = piece(part, p, s, k)
        c = pltpu.make_async_remote_copy(
            src_ref=r, dst_ref=r, send_sem=kv_send.at[len(sent)], recv_sem=rs,
            device_id=dev, device_id_type=MESH,
        )
        if cond is None:
            c.start()
        else:
            pl.when(cond)(c.start)
        sent.append((cond, c))

    def wait_for(cond, part, p, s, kk):
        r, rs = piece(part, p, s, kk)
        c = pltpu.make_async_remote_copy(
            src_ref=r, dst_ref=r, send_sem=kv_send.at[0], recv_sem=rs,
            device_id=sib, device_id_type=MESH,
        )
        if cond is None:
            c.wait_recv()
        else:
            pl.when(cond)(c.wait_recv)

    y0 = y == 0
    y1 = y == 1

    def up(kind, s, d):
        if kind == "KX":
            return y1
        low = s + d <= 7
        return jnp.logical_or(y0, low) if kind == "VO" else low

    def down(kind, s):
        if kind == "KX":
            return y1
        low = s <= 2
        return jnp.logical_or(y0, low) if kind == "VO" else low

    zero = jnp.int32(0)
    KINDS = (("KO", 0, y), ("VO", 1, y), ("KX", 0, zero))

    for part in (0, 1):
        kind = ("KO", "VO")[part]
        send(up(kind, z, 1), part, y, z, zplus)
        send(down(kind, z), part, y, z, zminus)
        send(y0, part, y, z, ypart)
        send(None, part, y, z, sib)

    loads[2].wait()
    q = jnp.dot(N[...], W[:, :H1], preferred_element_type=F32) + bq[...].astype(F32)
    for h in range(NH):
        Q[h] = rope(q[:, h * HD:(h + 1) * HD]).astype(BF)

    scale = HD ** (-0.5)

    def attend(p, s, diag):
        b0 = p * 16 + s * 2
        keys = Kb[pl.ds(b0, 2)].reshape(2 * T, HD)
        vals = Vb[pl.ds(b0, 2)].reshape(2 * T, HD)
        kpos = lax.broadcasted_iota(jnp.int32, (T, 2 * T), 1) + b0 * T
        allowed = kpos >= START[:, :1]
        if diag:
            qpos = lax.broadcasted_iota(jnp.int32, (T, 2 * T), 0) + cp * T
            allowed = jnp.logical_and(allowed, kpos <= qpos)
        for h in range(NH):
            sc = lax.dot_general(
                Q[h], keys, (((1,), (1,)), ((), ())), preferred_element_type=F32
            ) * scale
            sc = jnp.where(allowed, sc, NEG)
            top = jnp.max(sc, axis=1, keepdims=True)
            if not diag:
                top = jnp.maximum(top, M[h][:, :1])
            w = jnp.exp(sc - top)
            tot = w[:, :HD]
            for c in range(1, 2 * T // HD):
                tot = tot + w[:, c * HD:(c + 1) * HD]
            add = jnp.dot(w.astype(BF), vals, preferred_element_type=F32)
            if diag:
                L[h] = tot
                ACC[h] = add
            else:
                f = jnp.exp(M[h] - top)
                L[h] = L[h] * f + tot
                ACC[h] = ACC[h] * f + add
            M[h] = jnp.broadcast_to(top, (T, HD))

    def ring(d):
        s = lax.rem(z + 8 - d, 8)
        for kind, part, p in KINDS:
            got = up(kind, s, d)
            wait_for(got, part, p, s, k)
            if d < 4:
                send(up(kind, s, d + 1), part, p, s, zplus)
            if kind == "VO":
                send(y0, part, p, s, ypart)
            send(y1 if kind == "KX" else z - d >= 0, part, p, s, sib)
        if d < 4:
            s = lax.rem(z + d, 8)
            for kind, part, p in KINDS:
                got = down(kind, s)
                wait_for(got, part, p, s, k)
                if d < 3:
                    send(got, part, p, s, zminus)
                if kind == "VO":
                    send(y0, part, p, s, ypart)
                send(y1 if kind == "KX" else z + d >= 8, part, p, s, sib)

    def cross(d):
        for s in ([lax.rem(z + 8 - d, 8)] + ([lax.rem(z + d, 8)] if 0 < d < 4 else [])):
            wait_for(y1, 1, zero, s, k)
            send(y1, 1, zero, s, sib)

    def slabs(e, e2):
        def step(j, carry):
            i = lax.rem(j, 2)
            other = lax.div(j, 2)
            dist = e * (1 - other) + e2 * other
            v = z + (2 * i - 1) * dist
            s = lax.rem(v + 8, 8)
            p = y * (1 - other)
            two = lambda n: 0 < n < 4
            own_ok = v - 8 * i >= 0
            if not two(e):
                own_ok = jnp.logical_and(own_ok, i == 0) if e == 4 else (i < 0)
            oth_ok = y1
            if not two(e2):
                oth_ok = jnp.logical_and(y1, i == 0) if e2 in (0, 4) else (i < 0)
            cond = jnp.logical_or(
                jnp.logical_and(other == 0, own_ok), jnp.logical_and(other == 1, oth_ok)
            )

            @pl.when(cond)
            def _():
                wait_for(None, 0, p, s, 1 - k)
                wait_for(None, 1, p, s, 1 - k)
                attend(p, s, False)

            return carry

        lax.fori_loop(0, 4, step, 0)

    wait_for(y1, 0, zero, z, k)
    send(y1, 0, zero, z, zplus)
    send(y1, 0, zero, z, zminus)
    send(y1, 0, zero, z, sib)
    wait_for(None, 0, y, z, 1 - k)
    wait_for(None, 1, y, z, 1 - k)
    attend(y, z, True)
    for r in range(1, 7):
        if r <= 4:
            ring(r)
        if r <= 5:
            cross(r - 1)
        slabs(r - 1, r - 2)

    gc = Gather(AT, H1, c_send, c_recv)
    for h in range(NH):
        o = ACC[h] / jnp.sum(L[h], axis=1, keepdims=True)
        AT[:, pl.ds(pl.multiple_of(tp * H1 + h * HD, 128), HD)] = o.astype(BF)
    gc.start()
    loads[3].wait()
    OACC[...] = G[:, own_cols].astype(F32)

    def project(xi):
        rows = pl.ds(pl.multiple_of(xi * 2 * H1, 128), 2 * H1)
        OACC[...] += jnp.dot(AT[:, rows], Wo[rows, :], preferred_element_type=F32)

    gc.run([
        lambda: None,
        lambda: project(x),
        lambda: None,
        lambda: (project(xl), project(xr)),
        lambda: project(xo),
    ])
    mixed[...] = OACC[...].astype(BF)
    ga.drain()
    gc.drain()
    for cond, c in sent:
        if cond is None:
            c.wait_send()
        else:
            pl.when(cond)(c.wait_send)


def local(
    hidden_in, norm_gain, seq_lengths, w_query, b_query, w_key, b_key, w_value, b_value, w_out
):
    T, D1 = hidden_in.shape
    D = w_query.shape[0]
    H1 = w_query.shape[1]
    NH = H1 // HD
    f = ROPE_BASE ** (-jnp.arange(HD // 2, dtype=F32) / (HD // 2))
    freq = jnp.concatenate([f, f]).reshape(1, HD)
    vm = pl.BlockSpec(memory_space=pltpu.VMEM)
    hb = pl.BlockSpec(memory_space=pl.ANY)
    sm = pl.BlockSpec(memory_space=pltpu.SMEM)
    V = pltpu.VMEM
    return pl.pallas_call(
        kernel,
        out_shape=(
            jax.ShapeDtypeStruct((T, D1), BF),
            jax.ShapeDtypeStruct((T, HD), BF),
            jax.ShapeDtypeStruct((T, HD), BF),
        ),
        in_specs=[hb, vm, sm, hb, vm, hb, vm, hb, vm, hb, vm],
        out_specs=(vm, vm, vm),
        scratch_shapes=[
            V((T, D), BF), V((T, D), BF), V((D, H1 + 2 * HD), BF), V(w_out.shape, BF),
            V((32, T, HD), BF), V((32, T, HD), BF), V((T, 8 * H1), BF), V((NH, T, HD), BF),
            V((NH, T, HD), F32), V((NH, T, HD), F32), V((NH, T, HD), F32),
            V((T, HD), F32), V((T, HD), F32), V((T, HD), jnp.int32), V((T, HD), F32),
            V((T, D1), F32),
            pltpu.SemaphoreType.DMA((5,)),
            pltpu.SemaphoreType.DMA((14,)), pltpu.SemaphoreType.DMA((16,)),
            pltpu.SemaphoreType.DMA((14,)), pltpu.SemaphoreType.DMA((16,)),
            pltpu.SemaphoreType.DMA((SENDS,)), pltpu.SemaphoreType.DMA((64,)),
        ],
        compiler_params=pltpu.CompilerParams(
            collective_id=0, has_side_effects=True, vmem_limit_bytes=60 * 1024 * 1024
        ),
        name="layer",
    )(
        hidden_in, norm_gain.reshape(1, D), seq_lengths, w_query, b_query.reshape(1, H1),
        w_key, b_key.reshape(1, HD), w_value, b_value.reshape(1, HD), w_out, freq,
    )


def solution(mesh):
    placed = (
        P("cp", "tp"), P(), P(), P(None, "tp"), P("tp"), P(None, "tp"), P("tp"),
        P(None, "tp"), P("tp"), P(None, "tp"),
    )
    return jax.shard_map(
        local, mesh=mesh, in_specs=placed,
        out_specs=(P("cp", "tp"), P("cp", "tp"), P("cp", "tp")), check_vma=False,
    )
```

profile of v0, /device:TPU:232, one launch (start us, length us, event | category | flops | bytes accessed | tf_op | source)
XLA Modules:
  0.0 94.0 jit_solution(18313140721592608531)
XLA Ops:
  0.6 0.6 maximum_bitcast_fusion.freq
  1.2 1.2 %reshape.22.bq = bf16[1,384]{1,0:T(2,128)(2,1)} reshape(bf16[384]{0:T(512)(128)(2,1)} %param.14) | data formatting | bytes 1536 | tf_op jit(solution)/shard_map/reshape | solution.py:425
  2.5 86.8 %layer.1 = (bf16[256,640]{1,0:T(8,128)(2,1)}, bf16[256,128]{1,0:T(8,128)(2,1)}, bf16[256,128]{1,0:T(8,128)(2,1)}) custom-call(bf16[256,640]{1,0:T(8,128)(2,1)} %hid.1, f32[1,5120]{1,0:T(1,128)} %bitcast.5, s32[16]{0:T(128)} %seq.1, bf16[5120,384]{1,0:T(8,128)(2,1)} %wq.1, bf16[1,384]{1,0:T(2,128)(2,1)} %reshape.22.bq, bf16[5120,128]{1,0:T(8,128)(2,1)} %wk.1, ...), custom_call_target="tpu_custom_call" | custom-call | tf_op jit(solution)/shard_map/layer/pallas_call | solution.py:400
  89.3 1.7 %copy.16 = bf16[256,640]{1,0:T(8,128)(2,1)} copy(bf16[256,640]{1,0:T(8,128)(2,1)} %get-tuple-element.6) | data formatting | bytes 655360
  91.0 1.5 %copy.17 = bf16[256,128]{1,0:T(8,128)(2,1)} copy(bf16[256,128]{1,0:T(8,128)(2,1)} %get-tuple-element.7) | data formatting | bytes 131072
  92.5 1.5 %copy.18 = bf16[256,128]{1,0:T(8,128)(2,1)} copy(bf16[256,128]{1,0:T(8,128)(2,1)} %get-tuple-element.8) | data formatting | bytes 131072
  (1 shorter events, 0.0 us)
where the time goes:
time: 94.3 us; the launch traced here: 94 us
  Pallas kernels  86.8 us (92%)
  local copies, waits for them, and re-layouts  5.91 us (6%)
    pallas_call x1, Pallas kernels, local(): pl.pallas_call(kernel, out_shape=(jax.ShapeDtypeStruct((T, D1), BF), jax....  86.8 us
    unnamed x3, local copies, waits for them, and re-layouts  4.67 us

commit v1 on v0

--- a/solution.py
+++ b/solution.py
@@ -1,7 +1,6 @@
-import functools
-
 import jax
 import jax.numpy as jnp
+import numpy as np
 from jax import lax
 from jax.experimental import pallas as pl
 from jax.experimental.pallas import tpu as pltpu
@@ -10,7 +9,8 @@
 HD = 128
 EPS = 1e-06
 ROPE_BASE = 1000000.0
-NEG = -1e30
+FAR = -float(2**100)
+LOG2E = 1.4426950408889634
 MESH = pl.DeviceIdType.MESH
 BF = jnp.bfloat16
 F32 = jnp.float32
@@ -21,7 +21,7 @@
 def kernel(
     hid, gain, seq, wq, bq, wk, bk, wv, bv, wo, freq,
     mixed, kout, vout,
-    G, N, W, Wo, Kb, Vb, AT, Q, M, L, ACC, COS, SIN, START, SS, OACC,
+    G, N, W, Wo, Kb, Vb, AT, Q, M, L, ACC, COS, SIN, QDOC, DOC, SS, OACC,
     lsem, a_send, a_recv, c_send, c_recv, kv_send, kv_recv,
 ):
     T = hid.shape[0]
@@ -118,13 +118,13 @@
             self.wait(LEFT, 1)
             self.wait(RIGHT, 0)
             hooks[1]()
+            self.wait(OPP, 0)
+            self.send(OPP, 0, partner, POPP)
+            self.wait(OPP, 1)
+            self.send(OPP, 1, partner, POPP)
+            hooks[2]()
             self.wait(PLEFT, 0)
-            self.send(PLEFT, 0, right, POPP)
             self.wait(PRIGHT, 1)
-            self.send(PRIGHT, 1, left, POPP)
-            self.wait(OPP, 0)
-            self.wait(OPP, 1)
-            hooks[2]()
             self.wait(PLEFT, 1)
             self.wait(PRIGHT, 0)
             hooks[3]()
@@ -139,17 +139,32 @@
     ga = Gather(G, D1, a_send, a_recv)
     ga.start()
 
+    lane = lax.broadcasted_iota(jnp.int32, (1, HD), 1)
+    starts = jnp.full((1, HD), 1 << 30, jnp.int32)
+    ends = jnp.zeros((1, HD), jnp.int32)
     tok = lax.broadcasted_iota(jnp.int32, (T, HD), 0) + cp * T
     first = jnp.zeros((T, HD), jnp.int32)
-    run_start = jnp.int32(0)
+    edge = jnp.int32(0)
     for j in range(seq.shape[0]):
-        first = jnp.where(tok >= run_start, run_start, first)
-        run_start = run_start + seq[j]
-    START[...] = first
+        first = jnp.where(tok >= edge, edge, first)
+        starts = jnp.where(lane == j, edge, starts)
+        edge = edge + seq[j]
+        ends = jnp.where(lane == j, edge, ends)
     angle = (tok - first).astype(F32) * freq[...]
     COS[...] = jnp.cos(angle)
     sgn = jnp.where(lax.broadcasted_iota(jnp.int32, (T, HD), 1) < HD // 2, -1.0, 1.0)
     SIN[...] = jnp.sin(angle) * sgn
+    inside = jnp.logical_and(tok >= starts, tok < ends)
+    QDOC[...] = jnp.where(inside, FAR, 0.0).astype(BF)
+    live = lane < seq.shape[0]
+
+    def doc_block(i, carry):
+        pos = lax.broadcasted_iota(jnp.int32, (T, HD), 0) + i * T
+        out = jnp.logical_or(pos < starts, pos >= ends)
+        DOC[i] = jnp.where(jnp.logical_and(out, live), 1.0, 0.0).astype(BF)
+        return carry
+
+    lax.fori_loop(0, DOC.shape[0], doc_block, 0)
 
     def slab(slot):
         return pl.ds(pl.multiple_of(tps[slot] * D1, 128), D1)
@@ -232,11 +247,14 @@
         low = s + d <= 7
         return jnp.logical_or(y0, low) if kind == "VO" else low
 
-    def down(kind, s):
+    def down(kind, s, d):
         if kind == "KX":
-            return y1
+            return jnp.logical_and(y1, s - d >= 0)
         low = s <= 2
         return jnp.logical_or(y0, low) if kind == "VO" else low
+
+    def seen(s):
+        return s >= z - 4
 
     zero = jnp.int32(0)
     KINDS = (("KO", 0, y), ("VO", 1, y), ("KX", 0, zero))
@@ -244,35 +262,36 @@
     for part in (0, 1):
         kind = ("KO", "VO")[part]
         send(up(kind, z, 1), part, y, z, zplus)
-        send(down(kind, z), part, y, z, zminus)
+        send(down(kind, z, 1), part, y, z, zminus)
         send(y0, part, y, z, ypart)
         send(None, part, y, z, sib)
 
     loads[2].wait()
-    q = jnp.dot(N[...], W[:, :H1], preferred_element_type=F32) + bq[...].astype(F32)
+    q = jnp.dot(N[...], W[:, :H1], preferred_element_type=F32)
     for h in range(NH):
-        Q[h] = rope(q[:, h * HD:(h + 1) * HD]).astype(BF)
-
-    scale = HD ** (-0.5)
+        Q[h] = rope(q[:, h * HD:(h + 1) * HD] + bq[h:h + 1, :].astype(F32)).astype(BF)
+
+    scale = HD ** (-0.5) * LOG2E
 
     def attend(p, s, diag):
         b0 = p * 16 + s * 2
-        keys = Kb[pl.ds(b0, 2)].reshape(2 * T, HD)
+        keys = jnp.concatenate(
+            [Kb[pl.ds(b0, 2)].reshape(2 * T, HD), DOC[pl.ds(b0, 2)].reshape(2 * T, HD)], axis=1
+        )
         vals = Vb[pl.ds(b0, 2)].reshape(2 * T, HD)
-        kpos = lax.broadcasted_iota(jnp.int32, (T, 2 * T), 1) + b0 * T
-        allowed = kpos >= START[:, :1]
-        if diag:
-            qpos = lax.broadcasted_iota(jnp.int32, (T, 2 * T), 0) + cp * T
-            allowed = jnp.logical_and(allowed, kpos <= qpos)
         for h in range(NH):
             sc = lax.dot_general(
-                Q[h], keys, (((1,), (1,)), ((), ())), preferred_element_type=F32
-            ) * scale
-            sc = jnp.where(allowed, sc, NEG)
+                jnp.concatenate([Q[h], QDOC[...]], axis=1), keys, (((1,), (1,)), ((), ())),
+                preferred_element_type=F32,
+            )
+            if diag:
+                kpos = lax.broadcasted_iota(jnp.int32, (T, 2 * T), 1)
+                qpos = lax.broadcasted_iota(jnp.int32, (T, 2 * T), 0) + k * T
+                sc = jnp.where(kpos <= qpos, sc, FAR)
             top = jnp.max(sc, axis=1, keepdims=True)
             if not diag:
                 top = jnp.maximum(top, M[h][:, :1])
-            w = jnp.exp(sc - top)
+            w = jnp.exp2((sc - top) * scale)
             tot = w[:, :HD]
             for c in range(1, 2 * T // HD):
                 tot = tot + w[:, c * HD:(c + 1) * HD]
@@ -281,79 +300,73 @@
                 L[h] = tot
                 ACC[h] = add
             else:
-                f = jnp.exp(M[h] - top)
+                f = jnp.exp2((M[h] - top) * scale)
                 L[h] = L[h] * f + tot
                 ACC[h] = ACC[h] * f + add
             M[h] = jnp.broadcast_to(top, (T, HD))
 
-    def ring(d):
+    def plus(d):
         s = lax.rem(z + 8 - d, 8)
         for kind, part, p in KINDS:
-            got = up(kind, s, d)
-            wait_for(got, part, p, s, k)
+            wait_for(up(kind, s, d), part, p, s, k)
             if d < 4:
                 send(up(kind, s, d + 1), part, p, s, zplus)
             if kind == "VO":
-                send(y0, part, p, s, ypart)
+                send(jnp.logical_and(y0, seen(s)), part, p, s, ypart)
             send(y1 if kind == "KX" else z - d >= 0, part, p, s, sib)
-        if d < 4:
-            s = lax.rem(z + d, 8)
-            for kind, part, p in KINDS:
-                got = down(kind, s)
-                wait_for(got, part, p, s, k)
-                if d < 3:
-                    send(got, part, p, s, zminus)
-                if kind == "VO":
-                    send(y0, part, p, s, ypart)
-                send(y1 if kind == "KX" else z + d >= 8, part, p, s, sib)
-
-    def cross(d):
-        for s in ([lax.rem(z + 8 - d, 8)] + ([lax.rem(z + d, 8)] if 0 < d < 4 else [])):
-            wait_for(y1, 1, zero, s, k)
-            send(y1, 1, zero, s, sib)
-
-    def slabs(e, e2):
-        def step(j, carry):
-            i = lax.rem(j, 2)
-            other = lax.div(j, 2)
-            dist = e * (1 - other) + e2 * other
-            v = z + (2 * i - 1) * dist
-            s = lax.rem(v + 8, 8)
-            p = y * (1 - other)
-            two = lambda n: 0 < n < 4
-            own_ok = v - 8 * i >= 0
-            if not two(e):
-                own_ok = jnp.logical_and(own_ok, i == 0) if e == 4 else (i < 0)
-            oth_ok = y1
-            if not two(e2):
-                oth_ok = jnp.logical_and(y1, i == 0) if e2 in (0, 4) else (i < 0)
-            cond = jnp.logical_or(
-                jnp.logical_and(other == 0, own_ok), jnp.logical_and(other == 1, oth_ok)
-            )
-
-            @pl.when(cond)
-            def _():
-                wait_for(None, 0, p, s, 1 - k)
-                wait_for(None, 1, p, s, 1 - k)
-                attend(p, s, False)
-
-            return carry
-
-        lax.fori_loop(0, 4, step, 0)
+
+    def minus(d):
+        s = lax.rem(z + d, 8)
+        for kind, part, p in KINDS:
+            got = down(kind, s, d)
+            wait_for(got, part, p, s, k)
+            if d < 3:
+                send(down(kind, s, d + 1), part, p, s, zminus)
+            if kind == "VO":
+                send(jnp.logical_and(y0, seen(s)), part, p, s, ypart)
+            send(got if kind == "KX" else z + d >= 8, part, p, s, sib)
+
+    def cross(s):
+        here = jnp.logical_and(y1, seen(s))
+        wait_for(here, 1, zero, s, k)
+        send(here, 1, zero, s, sib)
+
+    def near(d):
+        return lax.rem(z + 8 - d, 8), lax.rem(z + d, 8)
+
+    def visit(cond, p, s):
+        @pl.when(cond)
+        def _():
+            wait_for(None, 0, p, s, 1 - k)
+            wait_for(None, 1, p, s, 1 - k)
+            attend(p, s, False)
 
     wait_for(y1, 0, zero, z, k)
     send(y1, 0, zero, z, zplus)
-    send(y1, 0, zero, z, zminus)
+    send(down("KX", z, 1), 0, zero, z, zminus)
     send(y1, 0, zero, z, sib)
     wait_for(None, 0, y, z, 1 - k)
     wait_for(None, 1, y, z, 1 - k)
     attend(y, z, True)
     for r in range(1, 7):
+        lo, hi = near(r - 1)
+        lo2, hi2 = near(max(r - 2, 0))
         if r <= 4:
-            ring(r)
+            plus(r)
+        if 2 <= r <= 5:
+            visit(z - (r - 1) >= 0, y, lo)
+        if r <= 3:
+            minus(r)
+        if 2 <= r <= 4:
+            visit(z + (r - 1) >= 8, y, hi)
         if r <= 5:
-            cross(r - 1)
-        slabs(r - 1, r - 2)
+            cross(lo)
+        if 2 <= r:
+            visit(jnp.logical_and(y1, seen(lo2)), zero, lo2)
+        if 2 <= r <= 4:
+            cross(hi)
+        if 3 <= r <= 5:
+            visit(jnp.logical_and(y1, seen(hi2)), zero, hi2)
 
     gc = Gather(AT, H1, c_send, c_recv)
     for h in range(NH):
@@ -384,6 +397,18 @@
             pl.when(cond)(c.wait_send)
 
 
+def finish(a, b, c, oa, ob, oc, va, vb, vc, sems):
+    ins = [pltpu.make_async_copy(r, v, sems.at[i]) for i, (r, v) in enumerate(((b, vb), (c, vc), (a, va)))]
+    outs = [pltpu.make_async_copy(v, o, sems.at[3 + i]) for i, (v, o) in enumerate(((vb, ob), (vc, oc), (va, oa)))]
+    for c_in in ins:
+        c_in.start()
+    for c_in, c_out in zip(ins, outs):
+        c_in.wait()
+        c_out.start()
+    for c_out in outs:
+        c_out.wait()
+
+
 def local(
     hidden_in, norm_gain, seq_lengths, w_query, b_query, w_key, b_key, w_value, b_value, w_out
 ):
@@ -391,13 +416,13 @@
     D = w_query.shape[0]
     H1 = w_query.shape[1]
     NH = H1 // HD
-    f = ROPE_BASE ** (-jnp.arange(HD // 2, dtype=F32) / (HD // 2))
-    freq = jnp.concatenate([f, f]).reshape(1, HD)
+    f = (ROPE_BASE ** (-np.arange(HD // 2) / (HD // 2))).astype(np.float32)
+    freq = jnp.asarray(np.concatenate([f, f]).reshape(1, HD))
     vm = pl.BlockSpec(memory_space=pltpu.VMEM)
     hb = pl.BlockSpec(memory_space=pl.ANY)
     sm = pl.BlockSpec(memory_space=pltpu.SMEM)
     V = pltpu.VMEM
-    return pl.pallas_call(
+    made = pl.pallas_call(
         kernel,
         out_shape=(
             jax.ShapeDtypeStruct((T, D1), BF),
@@ -410,7 +435,7 @@
             V((T, D), BF), V((T, D), BF), V((D, H1 + 2 * HD), BF), V(w_out.shape, BF),
             V((32, T, HD), BF), V((32, T, HD), BF), V((T, 8 * H1), BF), V((NH, T, HD), BF),
             V((NH, T, HD), F32), V((NH, T, HD), F32), V((NH, T, HD), F32),
-            V((T, HD), F32), V((T, HD), F32), V((T, HD), jnp.int32), V((T, HD), F32),
+            V((T, HD), F32), V((T, HD), F32), V((T, HD), BF), V((32, T, HD), BF), V((T, HD), F32),
             V((T, D1), F32),
             pltpu.SemaphoreType.DMA((5,)),
             pltpu.SemaphoreType.DMA((14,)), pltpu.SemaphoreType.DMA((16,)),
@@ -422,9 +447,17 @@
         ),
         name="layer",
     )(
-        hidden_in, norm_gain.reshape(1, D), seq_lengths, w_query, b_query.reshape(1, H1),
+        hidden_in, norm_gain.reshape(1, D), seq_lengths, w_query, b_query.reshape(NH, HD),
         w_key, b_key.reshape(1, HD), w_value, b_value.reshape(1, HD), w_out, freq,
     )
+    return pl.pallas_call(
+        finish,
+        out_shape=tuple(jax.ShapeDtypeStruct(m.shape, m.dtype) for m in made),
+        in_specs=[hb, hb, hb],
+        out_specs=(hb, hb, hb),
+        scratch_shapes=[V(m.shape, m.dtype) for m in made] + [pltpu.SemaphoreType.DMA((6,))],
+        name="finish",
+    )(*made)
 
 
 def solution(mesh):

time: 94.3 us -> 79 us (0.84)
  the two profiles are of different devices: /device:TPU:232 before, /device:TPU:24 now
where the time goes in v1:
time: 79 us; the launch traced here: 78.3 us
  Pallas kernels  77.5 us (98%)
  between operations  0.8 us (1%)
    pallas_call x1, Pallas kernels, local(): pl.pallas_call(kernel, out_shape=(jax.ShapeDtypeStruct((T, D1), BF), jax....  75.6 us
    pallas_call x1, Pallas kernels, local(): pl.pallas_call(finish, out_shape=tuple((jax.ShapeDtypeStruct(m.shape, m.d...  1.83 us

profile of v1, /device:TPU:24, one launch (start us, length us, event | category | flops | bytes accessed | tf_op | source)
XLA Modules:
  0.0 78.3 jit_solution(12974253080893251215)
XLA Ops:
  0.6 75.6 %layer.1 = (bf16[256,640]{1,0:T(8,128)(2,1)}, bf16[256,128]{1,0:T(8,128)(2,1)}, bf16[256,128]{1,0:T(8,128)(2,1)}) custom-call(bf16[256,640]{1,0:T(8,128)(2,1)} %hid.1, f32[1,5120]{1,0:T(1,128)} %bitcast.4, s32[16]{0:T(128)} %seq.1, bf16[5120,384]{1,0:T(8,128)(2,1)} %wq.1, bf16[3,128]{1,0:T(4,128)(2,1)} %bitcast.5, bf16[5120,128]{1,0:T(8,128)(2,1)} %wk.1, ...), custom_call_target="tpu_custom_call" | custom-call | tf_op jit(solution)/shard_map/layer/pallas_call | solution.py:425
  76.3 1.8 %finish.1 = (bf16[256,640]{1,0:T(8,128)(2,1)}, bf16[256,128]{1,0:T(8,128)(2,1)}, bf16[256,128]{1,0:T(8,128)(2,1)}) custom-call(bf16[256,640]{1,0:T(8,128)(2,1)} %get-tuple-element.6.a, bf16[256,128]{1,0:T(8,128)(2,1)} %get-tuple-element.7.b, bf16[256,128]{1,0:T(8,128)(2,1)} %get-tuple-element.8.c), custom_call_target="tpu_custom_call" | custom-call | tf_op jit(solution)/shard_map/finish/pallas_call | solution.py:453

commit v2 on v1

v2 whole, which is shorter than its diff:
```python
import jax
import jax.numpy as jnp
import numpy as np
from jax import lax
from jax.experimental import pallas as pl
from jax.experimental.pallas import tpu as pltpu
from jax.sharding import PartitionSpec as P

HD = 128
EPS = 1e-06
ROPE_BASE = 1000000.0
FAR = -float(2**100)
LOG2E = 1.4426950408889634
MESH = pl.DeviceIdType.MESH
BF = jnp.bfloat16
F32 = jnp.float32
LEFT, RIGHT, OPP, PART, PLEFT, PRIGHT, POPP = 1, 2, 3, 4, 5, 6, 7
SENDS = 72


def kernel(
    hid, gain_h, seq_h, wq, bq_h, wk, bk_h, wv, bv_h, wo, freq_h,
    mixed, kout, vout,
    gain, bq, bk, bv, freq, seq, G, N, W, Wo, Kb, Vb, AT, Q, M, L, ACC, COS, SIN, QDOC, DOC, SS, OACC,
    lsem, a_send, a_recv, c_send, c_recv, kv_send, kv_recv,
):
    T = hid.shape[0]
    D1 = hid.shape[1]
    H1 = wo.shape[0] // 8
    NH = H1 // HD
    cp = lax.axis_index("cp")
    tp = lax.axis_index("tp")
    y = lax.div(cp, 16)
    z = lax.div(lax.rem(cp, 16), 2)
    k = lax.rem(cp, 2)
    x = lax.div(tp, 2)
    yh = lax.rem(tp, 2)
    xl = lax.rem(x + 3, 4)
    xr = lax.rem(x + 1, 4)
    xo = lax.rem(x + 2, 4)
    right = (cp, 2 * xr + yh)
    left = (cp, 2 * xl + yh)
    partner = (cp, 2 * x + 1 - yh)
    zplus = (y * 16 + lax.rem(z + 1, 8) * 2 + k, tp)
    zminus = (y * 16 + lax.rem(z + 7, 8) * 2 + k, tp)
    ypart = ((1 - y) * 16 + z * 2 + k, tp)
    sib = (y * 16 + z * 2 + 1 - k, tp)

    own_cols = pl.ds(pl.multiple_of(tp * D1, 128), D1)
    load_hid = pltpu.make_async_copy(hid, G.at[:, own_cols], lsem.at[0])
    load_hid.start()
    loads = [
        pltpu.make_async_copy(wk, W.at[:, pl.ds(H1, HD)], lsem.at[1]),
        pltpu.make_async_copy(wv, W.at[:, pl.ds(H1 + HD, HD)], lsem.at[2]),
        pltpu.make_async_copy(wq, W.at[:, pl.ds(0, H1)], lsem.at[3]),
        pltpu.make_async_copy(wo, Wo, lsem.at[4]),
    ]
    small = [
        pltpu.make_async_copy(a, b, lsem.at[5 + i])
        for i, (a, b) in enumerate(
            ((seq_h, seq), (freq_h, freq), (gain_h, gain), (bq_h, bq), (bk_h, bk), (bv_h, bv))
        )
    ]

    barrier = pltpu.get_barrier_semaphore()
    for dev in (right, left, partner, zplus, zminus, ypart, sib):
        pl.semaphore_signal(barrier, inc=1, device_id=dev, device_id_type=MESH)
    for c in small + loads:
        c.start()
    pl.semaphore_wait(barrier, 7)
    load_hid.wait()

    tps = {
        0: 2 * x + yh, LEFT: 2 * xl + yh, RIGHT: 2 * xr + yh, OPP: 2 * xo + yh,
        PART: 2 * x + 1 - yh, PLEFT: 2 * xl + 1 - yh, PRIGHT: 2 * xr + 1 - yh, POPP: 2 * xo + 1 - yh,
    }

    class Gather:
        def __init__(self, buf, width, ssem, rsem):
            self.buf, self.width, self.ssem, self.rsem = buf, width, ssem, rsem
            self.sent = []

        def ref(self, slot, c):
            cols = pl.ds(pl.multiple_of(tps[slot] * self.width, 128), self.width)
            return self.buf.at[pl.ds(c * (T // 4), T // 4), cols]

        def send(self, slot, c, dev, dst_slot):
            r = self.ref(slot, c)
            cpy = pltpu.make_async_remote_copy(
                src_ref=r, dst_ref=r, send_sem=self.ssem.at[len(self.sent)],
                recv_sem=self.rsem.at[dst_slot * 4 + c], device_id=dev, device_id_type=MESH,
            )
            cpy.start()
            self.sent.append(cpy)

        def wait(self, slot, *chunks):
            for c in chunks:
                r = self.ref(slot, c)
                pltpu.make_async_remote_copy(
                    src_ref=r, dst_ref=r, send_sem=self.ssem.at[0],
                    recv_sem=self.rsem.at[slot * 4 + c], device_id=right, device_id_type=MESH,
                ).wait_recv()

        def start(self):
            for c in (0, 1, 2):
                self.send(0, c, right, LEFT)
                self.send(0, (c + 2) % 4, left, RIGHT)
                self.send(0, c, partner, PART)
            self.send(0, 3, partner, PART)

        def pass_on(self, first):
            up, dn = (0, 2) if first else (1, 3)
            self.wait(LEFT, up)
            self.send(LEFT, up, right, OPP)
            self.wait(RIGHT, dn)
            self.send(RIGHT, dn, left, OPP)

        def rest(self):
            self.send(0, 3, right, LEFT)
            self.send(0, 1, left, RIGHT)

        def part(self, c):
            self.wait(PART, c)
            self.send(PART, c, right, PLEFT)
            self.send(PART, c, left, PRIGHT)

        def across(self, first):
            for c in ((0, 2) if first else (1, 3)):
                self.wait(OPP, c)
                self.send(OPP, c, partner, POPP)

        def drain(self):
            for c in self.sent:
                c.wait_send()

    ga = Gather(G, D1, a_send, a_recv)
    ga.start()

    for c in small:
        c.wait()

    lane = lax.broadcasted_iota(jnp.int32, (1, HD), 1)
    starts = jnp.full((1, HD), 1 << 30, jnp.int32)
    ends = jnp.zeros((1, HD), jnp.int32)
    tok = lax.broadcasted_iota(jnp.int32, (T, HD), 0) + cp * T
    first = jnp.zeros((T, HD), jnp.int32)
    edge = jnp.int32(0)
    for j in range(seq.shape[0]):
        first = jnp.where(tok >= edge, edge, first)
        starts = jnp.where(lane == j, edge, starts)
        edge = edge + seq[j]
        ends = jnp.where(lane == j, edge, ends)
    angle = (tok - first).astype(F32) * freq[...]
    COS[...] = jnp.cos(angle)
    sgn = jnp.where(lax.broadcasted_iota(jnp.int32, (T, HD), 1) < HD // 2, -1.0, 1.0)
    SIN[...] = jnp.sin(angle) * sgn
    inside = jnp.logical_and(tok >= starts, tok < ends)
    QDOC[...] = jnp.where(inside, FAR, 0.0).astype(BF)
    live = lane < seq.shape[0]

    def doc_block(i, carry):
        pos = lax.broadcasted_iota(jnp.int32, (T, HD), 0) + i * T
        out = jnp.logical_or(pos < starts, pos >= ends)
        DOC[i] = jnp.where(jnp.logical_and(out, live), 1.0, 0.0).astype(BF)
        return carry

    lax.fori_loop(0, DOC.shape[0], doc_block, 0)

    def slab(slot):
        return pl.ds(pl.multiple_of(tps[slot] * D1, 128), D1)

    def squares(slots, init=False):
        total = None if init else SS[...]
        for s in slots:
            v = G[:, slab(s)].astype(F32)
            v = v * v
            for c in range(D1 // HD):
                piece = v[:, c * HD:(c + 1) * HD]
                total = piece if total is None else total + piece
        SS[...] = total

    def rope(u):
        return u * COS[...] + pltpu.roll(u, HD // 2, 1) * SIN[...]

    def keys_values():
        inv = lax.rsqrt(jnp.sum(SS[...], axis=1, keepdims=True) / (8.0 * D1) + EPS)
        pair = 2 * D1
        kv = None
        for i in range(4):
            sl = slice(i * pair, (i + 1) * pair)
            n = (G[:, sl].astype(F32) * inv * gain[:, sl]).astype(BF)
            N[:, sl] = n
            part = jnp.dot(n, W[sl, H1:], preferred_element_type=F32)
            kv = part if kv is None else kv + part
        knew = rope(kv[:, :HD] + bk[...].astype(F32)).astype(BF)
        vnew = (kv[:, HD:] + bv[...].astype(F32)).astype(BF)
        Kb[cp] = knew
        Vb[cp] = vnew
        kout[...] = knew
        vout[...] = vnew

    def queries():
        q = jnp.dot(N[...], W[:, :H1], preferred_element_type=F32)
        for h in range(NH):
            Q[h] = rope(q[:, h * HD:(h + 1) * HD] + bq[h:h + 1, :].astype(F32)).astype(BF)

    sent = []

    def piece(part, p, s, kk):
        blk = p * 16 + s * 2 + kk
        return (Kb if part == 0 else Vb).at[blk], kv_recv.at[part * 32 + blk]

    def send(cond, part, p, s, dev):
        r, rs = piece(part, p, s, k)
        c = pltpu.make_async_remote_copy(
            src_ref=r, dst_ref=r, send_sem=kv_send.at[len(sent)], recv_sem=rs,
            device_id=dev, device_id_type=MESH,
        )
        if cond is None:
            c.start()
        else:
            pl.when(cond)(c.start)
        sent.append((cond, c))

    def wait_for(cond, part, p, s, kk):
        r, rs = piece(part, p, s, kk)
        c = pltpu.make_async_remote_copy(
            src_ref=r, dst_ref=r, send_sem=kv_send.at[0], recv_sem=rs,
            device_id=sib, device_id_type=MESH,
        )
        if cond is None:
            c.wait_recv()
        else:
            pl.when(cond)(c.wait_recv)

    scale = HD ** (-0.5) * LOG2E

    def attend(p, s, diag):
        b0 = p * 16 + s * 2
        keys = jnp.concatenate(
            [Kb[pl.ds(b0, 2)].reshape(2 * T, HD), DOC[pl.ds(b0, 2)].reshape(2 * T, HD)], axis=1
        )
        vals = Vb[pl.ds(b0, 2)].reshape(2 * T, HD)
        qs = jnp.concatenate([jnp.concatenate([Q[h], QDOC[...]], axis=1) for h in range(NH)], axis=0)
        sc = lax.dot_general(qs, keys, (((1,), (1,)), ((), ())), preferred_element_type=F32)
        if diag:
            kpos = lax.broadcasted_iota(jnp.int32, (T, 2 * T), 1)
            qpos = lax.broadcasted_iota(jnp.int32, (T, 2 * T), 0) + k * T
            sc = jnp.concatenate([jnp.where(kpos <= qpos, sc[h * T:(h + 1) * T], FAR) for h in range(NH)], axis=0)
        top = jnp.max(sc, axis=1, keepdims=True)
        m_old = M[...].reshape(NH * T, HD)
        if not diag:
            top = jnp.maximum(top, m_old[:, :1])
        w = jnp.exp2((sc - top) * scale)
        tot = w[:, :HD]
        for c in range(1, 2 * T // HD):
            tot = tot + w[:, c * HD:(c + 1) * HD]
        add = jnp.dot(w.astype(BF), vals, preferred_element_type=F32)
        if not diag:
            f = jnp.exp2((m_old - top) * scale)
            tot = L[...].reshape(NH * T, HD) * f + tot
            add = ACC[...].reshape(NH * T, HD) * f + add
        L[...] = tot.reshape(NH, T, HD)
        ACC[...] = add.reshape(NH, T, HD)
        M[...] = jnp.broadcast_to(top, (NH * T, HD)).reshape(NH, T, HD)

    y0 = y == 0
    y1 = y == 1
    zero = jnp.int32(0)
    KINDS = (("KO", 0, y), ("VO", 1, y), ("KX", 0, zero))

    def up(kind, s, d):
        low = s + d <= 7
        if kind == "KX":
            return y1 if d <= 4 else None
        if kind == "KO":
            return low if d <= 3 else None
        return jnp.logical_or(y0, low) if d <= 3 else (y0 if d == 4 else None)

    def down(kind, s, d):
        if kind == "KX":
            return jnp.logical_and(y1, s - d >= 0) if d <= 3 else None
        if kind == "KO":
            return s <= 3 if d <= 4 else None
        return jnp.logical_or(y0, s <= 3) if d <= 3 else (jnp.logical_and(y1, s <= 3) if d == 4 else None)

    def seen(s):
        return s >= z - 4

    def own():
        for part in (0, 1):
            kind = ("KO", "VO")[part]
            send(up(kind, z, 1), part, y, z, zplus)
            send(down(kind, z, 1), part, y, z, zminus)
            send(y0, part, y, z, ypart)
            send(None, part, y, z, sib)

    def first_key():
        wait_for(y1, 0, zero, z, k)
        send(y1, 0, zero, z, zplus)
        send(down("KX", z, 1), 0, zero, z, zminus)
        send(y1, 0, zero, z, sib)

    def hop(d, step, go, dev, mine):
        s = lax.rem(z + 8 + step * d, 8)
        for kind, part, p in KINDS:
            got = go(kind, s, d)
            if got is None:
                continue
            wait_for(got, part, p, s, k)
            on = go(kind, s, d + 1)
            if on is not None:
                send(on, part, p, s, dev)
            if kind == "VO" and (d <= 3 or step < 0):
                send(jnp.logical_and(y0, seen(s)), part, p, s, ypart)
            send(got if kind == "KX" else jnp.logical_and(got, mine), part, p, s, sib)

    def plus(d):
        hop(d, -1, up, zplus, z - d >= 0)

    def minus(d):
        hop(d, 1, down, zminus, z + d >= 8)

    def cross(s):
        here = jnp.logical_and(y1, seen(s))
        wait_for(here, 1, zero, s, k)
        send(here, 1, zero, s, sib)

    def lo(d):
        return lax.rem(z + 8 - d, 8)

    def hi(d):
        return lax.rem(z + d, 8)

    def visit(cond, p, s):
        @pl.when(cond)
        def _():
            wait_for(None, 0, p, s, 1 - k)
            wait_for(None, 1, p, s, 1 - k)
            attend(p, s, False)

    ga.pass_on(True)
    ga.rest()
    squares((0,), True)
    ga.pass_on(False)
    ga.part(0)
    ga.part(1)
    ga.across(True)
    ga.part(2)
    ga.part(3)
    ga.wait(LEFT, 2, 3)
    ga.wait(RIGHT, 0, 1)
    squares((LEFT, RIGHT))
    ga.across(False)
    squares((PART, OPP))
    ga.wait(PLEFT, 0, 1, 2, 3)
    ga.wait(PRIGHT, 0, 1, 2, 3)
    squares((PLEFT, PRIGHT))
    ga.wait(POPP, 0, 1, 2, 3)
    squares((POPP,))
    loads[0].wait()
    loads[1].wait()
    keys_values()
    own()
    loads[2].wait()
    queries()
    first_key()
    wait_for(None, 0, y, z, 1 - k)
    wait_for(None, 1, y, z, 1 - k)
    attend(y, z, True)
    plus(1)
    minus(1)
    cross(z)
    plus(2)
    visit(z - 1 >= 0, y, lo(1))
    minus(2)
    visit(z + 1 >= 8, y, hi(1))
    cross(lo(1))
    visit(y1, zero, z)
    cross(hi(1))
    plus(3)
    visit(z - 2 >= 0, y, lo(2))
    minus(3)
    visit(z + 2 >= 8, y, hi(2))
    cross(lo(2))
    visit(jnp.logical_and(y1, seen(lo(1))), zero, lo(1))
    cross(hi(2))
    visit(jnp.logical_and(y1, seen(hi(1))), zero, hi(1))
    plus(4)
    visit(z - 3 >= 0, y, lo(3))
    minus(4)
    visit(z + 3 >= 8, y, hi(3))
    cross(lo(3))
    visit(jnp.logical_and(y1, seen(lo(2))), zero, lo(2))
    cross(hi(3))
    visit(jnp.logical_and(y1, seen(hi(2))), zero, hi(2))
    cross(lo(4))
    visit(z + 4 >= 8, y, hi(4))
    visit(jnp.logical_and(y1, seen(lo(3))), zero, lo(3))
    visit(jnp.logical_and(y1, seen(hi(3))), zero, hi(3))
    visit(jnp.logical_and(y1, seen(lo(4))), zero, lo(4))

    gc = Gather(AT, H1, c_send, c_recv)
    for h in range(NH):
        o = ACC[h] / jnp.sum(L[h], axis=1, keepdims=True)
        AT[:, pl.ds(pl.multiple_of(tp * H1 + h * HD, 128), HD)] = o.astype(BF)
    gc.start()
    loads[3].wait()
    OACC[...] = G[:, own_cols].astype(F32)

    def project(xi):
        rows = pl.ds(pl.multiple_of(xi * 2 * H1, 128), 2 * H1)
        OACC[...] += jnp.dot(AT[:, rows], Wo[rows, :], preferred_element_type=F32)

    gc.pass_on(True)
    gc.rest()
    gc.pass_on(False)
    gc.part(0)
    gc.part(1)
    gc.across(True)
    gc.part(2)
    gc.part(3)
    project(x)
    gc.across(False)
    gc.wait(LEFT, 2, 3)
    gc.wait(RIGHT, 0, 1)
    gc.wait(PLEFT, 0, 1, 2, 3)
    gc.wait(PRIGHT, 0, 1, 2, 3)
    project(xl)
    project(xr)
    gc.wait(POPP, 0, 1, 2, 3)
    project(xo)
    mixed[...] = OACC[...].astype(BF)
    ga.drain()
    gc.drain()
    for cond, c in sent:
        if cond is None:
            c.wait_send()
        else:
            pl.when(cond)(c.wait_send)


def finish(a, b, c, oa, ob, oc, va, vb, vc, sems):
    ins = [pltpu.make_async_copy(r, v, sems.at[i]) for i, (r, v) in enumerate(((b, vb), (c, vc), (a, va)))]
    outs = [pltpu.make_async_copy(v, o, sems.at[3 + i]) for i, (v, o) in enumerate(((vb, ob), (vc, oc), (va, oa)))]
    for c_in in ins:
        c_in.start()
    for c_in, c_out in zip(ins, outs):
        c_in.wait()
        c_out.start()
    for c_out in outs:
        c_out.wait()


def local(
    hidden_in, norm_gain, seq_lengths, w_query, b_query, w_key, b_key, w_value, b_value, w_out
):
    T, D1 = hidden_in.shape
    D = w_query.shape[0]
    H1 = w_query.shape[1]
    NH = H1 // HD
    f = (ROPE_BASE ** (-np.arange(HD // 2) / (HD // 2))).astype(np.float32)
    freq = jnp.asarray(np.concatenate([f, f]).reshape(1, HD))
    vm = pl.BlockSpec(memory_space=pltpu.VMEM)
    hb = pl.BlockSpec(memory_space=pl.ANY)
    V = pltpu.VMEM
    made = pl.pallas_call(
        kernel,
        out_shape=(
            jax.ShapeDtypeStruct((T, D1), BF),
            jax.ShapeDtypeStruct((T, HD), BF),
            jax.ShapeDtypeStruct((T, HD), BF),
        ),
        in_specs=[hb] * 11,
        out_specs=(vm, vm, vm),
        scratch_shapes=[
            V((1, D), F32), V((NH, HD), BF), V((1, HD), BF), V((1, HD), BF), V((1, HD), F32),
            pltpu.SMEM(seq_lengths.shape, jnp.int32),
            V((T, D), BF), V((T, D), BF), V((D, H1 + 2 * HD), BF), V(w_out.shape, BF),
            V((32, T, HD), BF), V((32, T, HD), BF), V((T, 8 * H1), BF), V((NH, T, HD), BF),
            V((NH, T, HD), F32), V((NH, T, HD), F32), V((NH, T, HD), F32),
            V((T, HD), F32), V((T, HD), F32), V((T, HD), BF), V((32, T, HD), BF), V((T, HD), F32),
            V((T, D1), F32),
            pltpu.SemaphoreType.DMA((11,)),
            pltpu.SemaphoreType.DMA((28,)), pltpu.SemaphoreType.DMA((32,)),
            pltpu.SemaphoreType.DMA((28,)), pltpu.SemaphoreType.DMA((32,)),
            pltpu.SemaphoreType.DMA((SENDS,)), pltpu.SemaphoreType.DMA((64,)),
        ],
        compiler_params=pltpu.CompilerParams(
            collective_id=0, has_side_effects=True, vmem_limit_bytes=60 * 1024 * 1024
        ),
        name="layer",
    )(
        hidden_in, norm_gain.reshape(1, D), seq_lengths, w_query, b_query.reshape(NH, HD),
        w_key, b_key.reshape(1, HD), w_value, b_value.reshape(1, HD), w_out, freq,
    )
    return pl.pallas_call(
        finish,
        out_shape=tuple(jax.ShapeDtypeStruct(m.shape, m.dtype) for m in made),
        in_specs=[hb, hb, hb],
        out_specs=(hb, hb, hb),
        scratch_shapes=[V(m.shape, m.dtype) for m in made] + [pltpu.SemaphoreType.DMA((6,))],
        name="finish",
    )(*made)


def solution(mesh):
    placed = (
        P("cp", "tp"), P(), P(), P(None, "tp"), P("tp"), P(None, "tp"), P("tp"),
        P(None, "tp"), P("tp"), P(None, "tp"),
    )
    return jax.shard_map(
        local, mesh=mesh, in_specs=placed,
        out_specs=(P("cp", "tp"), P("cp", "tp"), P("cp", "tp")), check_vma=False,
    )
```

time: 79 us -> 75 us (0.949)
  Pallas kernels: 77.5 us -> 74.1 us
    pallas_call x1, Pallas kernels: 75.6 us -> 72.3 us  [local(): pl.pallas_call(kernel, out_shape=(jax.ShapeDtypeStruct((T, D1), BF), jax....]
where the time goes in v2:
time: 75 us; the launch traced here: 74.9 us
  Pallas kernels  74.1 us (99%)
  between operations  0.8 us (1%)
    pallas_call x1, Pallas kernels, local(): pl.pallas_call(kernel, out_shape=(jax.ShapeDtypeStruct((T, D1), BF), jax....  72.3 us
    pallas_call x1, Pallas kernels, local(): pl.pallas_call(finish, out_shape=tuple((jax.ShapeDtypeStruct(m.shape, m.d...  1.83 us

profile of v2, /device:TPU:24, one launch (start us, length us, event | category | flops | bytes accessed | tf_op | source)
XLA Modules:
  0.0 74.9 jit_solution(17062398316697539558)
XLA Ops:
  0.6 72.3 %layer.1 = (bf16[256,640]{1,0:T(8,128)(2,1)}, bf16[256,128]{1,0:T(8,128)(2,1)}, bf16[256,128]{1,0:T(8,128)(2,1)}) custom-call(bf16[256,640]{1,0:T(8,128)(2,1)} %hid.1, f32[1,5120]{1,0:T(1,128)} %bitcast.4, s32[16]{0:T(128)} %seq_h.1, bf16[5120,384]{1,0:T(8,128)(2,1)} %wq.1, bf16[3,128]{1,0:T(4,128)(2,1)} %bitcast.5, bf16[5120,128]{1,0:T(8,128)(2,1)} %wk.1, ...), custom_call_target="tpu_custom_call" | custom-call | tf_op jit(solution)/shard_map/layer/pallas_call | solution.py:467
  72.9 1.8 %finish.1 = (bf16[256,640]{1,0:T(8,128)(2,1)}, bf16[256,128]{1,0:T(8,128)(2,1)}, bf16[256,128]{1,0:T(8,128)(2,1)}) custom-call(bf16[256,640]{1,0:T(8,128)(2,1)} %get-tuple-element.6.a, bf16[256,128]{1,0:T(8,128)(2,1)} %get-tuple-element.7.b, bf16[256,128]{1,0:T(8,128)(2,1)} %get-tuple-element.8.c), custom_call_target="tpu_custom_call" | custom-call | tf_op jit(solution)/shard_map/finish/pallas_call | solution.py:497

commit v3 on v2

--- a/solution.py
+++ b/solution.py
@@ -21,7 +21,7 @@
 def kernel(
     hid, gain_h, seq_h, wq, bq_h, wk, bk_h, wv, bv_h, wo, freq_h,
     mixed, kout, vout,
-    gain, bq, bk, bv, freq, seq, G, N, W, Wo, Kb, Vb, AT, Q, M, L, ACC, COS, SIN, QDOC, DOC, SS, OACC,
+    gain, bq, bk, bv, freq, seq, G, N, W, Wo, Kb, Vb, AT, Q, M, L, ACC, COS, SIN, QDOC, DOC, SS, OACC, MIX,
     lsem, a_send, a_recv, c_send, c_recv, kv_send, kv_recv,
 ):
     T = hid.shape[0]
@@ -45,10 +45,15 @@
     zminus = (y * 16 + lax.rem(z + 7, 8) * 2 + k, tp)
     ypart = ((1 - y) * 16 + z * 2 + k, tp)
     sib = (y * 16 + z * 2 + 1 - k, tp)
+    diag = ((1 - y) * 16 + lax.rem(z + 1 + 6 * y, 8) * 2 + k, tp)
 
     own_cols = pl.ds(pl.multiple_of(tp * D1, 128), D1)
-    load_hid = pltpu.make_async_copy(hid, G.at[:, own_cols], lsem.at[0])
-    load_hid.start()
+    quarters = [pl.ds(i * (T // 4), T // 4) for i in range(4)]
+    load_hid = [
+        pltpu.make_async_copy(hid.at[q, :], G.at[q, own_cols], lsem.at[11 + i]) for i, q in enumerate(quarters)
+    ]
+    for c in load_hid:
+        c.start()
     loads = [
         pltpu.make_async_copy(wk, W.at[:, pl.ds(H1, HD)], lsem.at[1]),
         pltpu.make_async_copy(wv, W.at[:, pl.ds(H1 + HD, HD)], lsem.at[2]),
@@ -62,13 +67,21 @@
         )
     ]
 
+    written = [
+        pltpu.make_async_copy(Kb.at[cp], kout, lsem.at[15]),
+        pltpu.make_async_copy(Vb.at[cp], vout, lsem.at[16]),
+    ] + [
+        pltpu.make_async_copy(MIX.at[q, :], mixed.at[q, :], lsem.at[17 + i]) for i, q in enumerate(quarters)
+    ]
+
     barrier = pltpu.get_barrier_semaphore()
-    for dev in (right, left, partner, zplus, zminus, ypart, sib):
+    for dev in (right, left, partner, zplus, zminus, ypart, sib, diag):
         pl.semaphore_signal(barrier, inc=1, device_id=dev, device_id_type=MESH)
     for c in small + loads:
         c.start()
-    pl.semaphore_wait(barrier, 7)
-    load_hid.wait()
+    pl.semaphore_wait(barrier, 8)
+    for c in load_hid:
+        c.wait()
 
     tps = {
         0: 2 * x + yh, LEFT: 2 * xl + yh, RIGHT: 2 * xr + yh, OPP: 2 * xo + yh,
@@ -196,8 +209,8 @@
         vnew = (kv[:, HD:] + bv[...].astype(F32)).astype(BF)
         Kb[cp] = knew
         Vb[cp] = vnew
-        kout[...] = knew
-        vout[...] = vnew
+        for c in written[:2]:
+            c.start()
 
     def queries():
         q = jnp.dot(N[...], W[:, :H1], preferred_element_type=F32)
@@ -275,7 +288,7 @@
             return y1 if d <= 4 else None
         if kind == "KO":
             return low if d <= 3 else None
-        return jnp.logical_or(y0, low) if d <= 3 else (y0 if d == 4 else None)
+        return jnp.logical_or(y0, low) if d <= 3 else (jnp.logical_and(y0, low) if d == 4 else None)
 
     def down(kind, s, d):
         if kind == "KX":
@@ -292,12 +305,13 @@
             kind = ("KO", "VO")[part]
             send(up(kind, z, 1), part, y, z, zplus)
             send(down(kind, z, 1), part, y, z, zminus)
+            if part == 0:
+                send(y0, part, y, z, diag)
             send(y0, part, y, z, ypart)
             send(None, part, y, z, sib)
 
     def first_key():
         wait_for(y1, 0, zero, z, k)
-        send(y1, 0, zero, z, zplus)
         send(down("KX", z, 1), 0, zero, z, zminus)
         send(y1, 0, zero, z, sib)
 
@@ -311,7 +325,9 @@
             on = go(kind, s, d + 1)
             if on is not None:
                 send(on, part, p, s, dev)
-            if kind == "VO" and (d <= 3 or step < 0):
+            if kind == "VO" and step < 0 and d == 3:
+                send(y0, part, p, s, diag)
+            if kind == "VO" and d <= 3:
                 send(jnp.logical_and(y0, seen(s)), part, p, s, ypart)
             send(got if kind == "KX" else jnp.logical_and(got, mine), part, p, s, sib)
 
@@ -394,9 +410,9 @@
     visit(jnp.logical_and(y1, seen(lo(2))), zero, lo(2))
     cross(hi(3))
     visit(jnp.logical_and(y1, seen(hi(2))), zero, hi(2))
-    cross(lo(4))
     visit(z + 4 >= 8, y, hi(4))
     visit(jnp.logical_and(y1, seen(lo(3))), zero, lo(3))
+    cross(lo(4))
     visit(jnp.logical_and(y1, seen(hi(3))), zero, hi(3))
     visit(jnp.logical_and(y1, seen(lo(4))), zero, lo(4))
 
@@ -420,8 +436,8 @@
     gc.across(True)
     gc.part(2)
     gc.part(3)
+    gc.across(False)
     project(x)
-    gc.across(False)
     gc.wait(LEFT, 2, 3)
     gc.wait(RIGHT, 0, 1)
     gc.wait(PLEFT, 0, 1, 2, 3)
@@ -429,10 +445,17 @@
     project(xl)
     project(xr)
     gc.wait(POPP, 0, 1, 2, 3)
-    project(xo)
-    mixed[...] = OACC[...].astype(BF)
+    rows = pl.ds(pl.multiple_of(xo * 2 * H1, 128), 2 * H1)
+    for i in (0, 2):
+        part = pl.ds(i * (T // 4), T // 2)
+        added = jnp.dot(AT[part, rows], Wo[rows, :], preferred_element_type=F32)
+        MIX[part, :] = (OACC[part, :] + added).astype(BF)
+        for c in written[2 + i:4 + i]:
+            c.start()
     ga.drain()
     gc.drain()
+    for c in written:
+        c.wait()
     for cond, c in sent:
         if cond is None:
             c.wait_send()
@@ -441,15 +464,19 @@
 
 
 def finish(a, b, c, oa, ob, oc, va, vb, vc, sems):
-    ins = [pltpu.make_async_copy(r, v, sems.at[i]) for i, (r, v) in enumerate(((b, vb), (c, vc), (a, va)))]
-    outs = [pltpu.make_async_copy(v, o, sems.at[3 + i]) for i, (v, o) in enumerate(((vb, ob), (vc, oc), (va, oa)))]
-    for c_in in ins:
-        c_in.start()
+    parts = 4
+    step = a.shape[0] // parts
+    moves = [(b, vb, ob), (c, vc, oc)]
+    moves += [tuple(r.at[pl.ds(i * step, step), :] for r in (a, va, oa)) for i in range(parts)]
+    ins = [pltpu.make_async_copy(r, v, sems.at[i]) for i, (r, v, o) in enumerate(moves)]
+    outs = [pltpu.make_async_copy(v, o, sems.at[len(moves) + i]) for i, (r, v, o) in enumerate(moves)]
+    for cpy in ins:
+        cpy.start()
     for c_in, c_out in zip(ins, outs):
         c_in.wait()
         c_out.start()
-    for c_out in outs:
-        c_out.wait()
+    for cpy in outs:
+        cpy.wait()
 
 
 def local(
@@ -472,7 +499,7 @@
             jax.ShapeDtypeStruct((T, HD), BF),
         ),
         in_specs=[hb] * 11,
-        out_specs=(vm, vm, vm),
+        out_specs=(hb, hb, hb),
         scratch_shapes=[
             V((1, D), F32), V((NH, HD), BF), V((1, HD), BF), V((1, HD), BF), V((1, HD), F32),
             pltpu.SMEM(seq_lengths.shape, jnp.int32),
@@ -480,8 +507,8 @@
             V((32, T, HD), BF), V((32, T, HD), BF), V((T, 8 * H1), BF), V((NH, T, HD), BF),
             V((NH, T, HD), F32), V((NH, T, HD), F32), V((NH, T, HD), F32),
             V((T, HD), F32), V((T, HD), F32), V((T, HD), BF), V((32, T, HD), BF), V((T, HD), F32),
-            V((T, D1), F32),
-            pltpu.SemaphoreType.DMA((11,)),
+            V((T, D1), F32), V((T, D1), BF),
+            pltpu.SemaphoreType.DMA((21,)),
             pltpu.SemaphoreType.DMA((28,)), pltpu.SemaphoreType.DMA((32,)),
             pltpu.SemaphoreType.DMA((28,)), pltpu.SemaphoreType.DMA((32,)),
             pltpu.SemaphoreType.DMA((SENDS,)), pltpu.SemaphoreType.DMA((64,)),
@@ -499,7 +526,7 @@
         out_shape=tuple(jax.ShapeDtypeStruct(m.shape, m.dtype) for m in made),
         in_specs=[hb, hb, hb],
         out_specs=(hb, hb, hb),
-        scratch_shapes=[V(m.shape, m.dtype) for m in made] + [pltpu.SemaphoreType.DMA((6,))],
+        scratch_shapes=[V(m.shape, m.dtype) for m in made] + [pltpu.SemaphoreType.DMA((12,))],
         name="finish",
     )(*made)
 

time: 75 us -> 74.6 us (level)
  no operation moved by 1% of the time
where the time goes in v3:
time: 74.6 us; the launch traced here: 74.4 us
  Pallas kernels  73.6 us (99%)
  between operations  0.8 us (1%)
    pallas_call x1, Pallas kernels, local(): pl.pallas_call(kernel, out_shape=(jax.ShapeDtypeStruct((T, D1), BF), jax....  71.8 us
    pallas_call x1, Pallas kernels, local(): pl.pallas_call(finish, out_shape=tuple((jax.ShapeDtypeStruct(m.shape, m.d...  1.82 us

profile of v3, /device:TPU:24, one launch (start us, length us, event | category | flops | bytes accessed | tf_op | source)
XLA Modules:
  0.0 74.4 jit_solution(9554327274589146564)
XLA Ops:
  0.6 71.8 %layer.1 = (bf16[256,640]{1,0:T(8,128)(2,1)}, bf16[256,128]{1,0:T(8,128)(2,1)}, bf16[256,128]{1,0:T(8,128)(2,1)}) custom-call(bf16[256,640]{1,0:T(8,128)(2,1)} %hid.1, f32[1,5120]{1,0:T(1,128)} %bitcast.4, s32[16]{0:T(128)} %seq_h.1, bf16[5120,384]{1,0:T(8,128)(2,1)} %wq.1, bf16[3,128]{1,0:T(4,128)(2,1)} %bitcast.5, bf16[5120,128]{1,0:T(8,128)(2,1)} %wk.1, ...), custom_call_target="tpu_custom_call" | custom-call | tf_op jit(solution)/shard_map/layer/pallas_call | solution.py:494
  72.5 1.8 %finish.1 = (bf16[256,640]{1,0:T(8,128)(2,1)}, bf16[256,128]{1,0:T(8,128)(2,1)}, bf16[256,128]{1,0:T(8,128)(2,1)}) custom-call(bf16[256,640]{1,0:T(8,128)(2,1)} %get-tuple-element.6.a, bf16[256,128]{1,0:T(8,128)(2,1)} %get-tuple-element.7.b, bf16[256,128]{1,0:T(8,128)(2,1)} %get-tuple-element.8.c), custom_call_target="tpu_custom_call" | custom-call | tf_op jit(solution)/shard_map/finish/pallas_call | solution.py:524

commit v4 on v3

--- a/solution.py
+++ b/solution.py
@@ -410,9 +410,9 @@
     visit(jnp.logical_and(y1, seen(lo(2))), zero, lo(2))
     cross(hi(3))
     visit(jnp.logical_and(y1, seen(hi(2))), zero, hi(2))
+    cross(lo(4))
     visit(z + 4 >= 8, y, hi(4))
     visit(jnp.logical_and(y1, seen(lo(3))), zero, lo(3))
-    cross(lo(4))
     visit(jnp.logical_and(y1, seen(hi(3))), zero, hi(3))
     visit(jnp.logical_and(y1, seen(lo(4))), zero, lo(4))
 

time: 74.6 us -> 74.3 us (level)
  no operation moved by 1% of the time
where the time goes in v4:
time: 74.3 us; the launch traced here: 74.1 us
  Pallas kernels  73.3 us (99%)
  between operations  0.8 us (1%)
    pallas_call x1, Pallas kernels, local(): pl.pallas_call(kernel, out_shape=(jax.ShapeDtypeStruct((T, D1), BF), jax....  71.5 us
    pallas_call x1, Pallas kernels, local(): pl.pallas_call(finish, out_shape=tuple((jax.ShapeDtypeStruct(m.shape, m.d...  1.82 us

profile of v4, /device:TPU:24, one launch (start us, length us, event | category | flops | bytes accessed | tf_op | source)
XLA Modules:
  0.0 74.1 jit_solution(6832090378722114688)
XLA Ops:
  0.6 71.5 %layer.1 = (bf16[256,640]{1,0:T(8,128)(2,1)}, bf16[256,128]{1,0:T(8,128)(2,1)}, bf16[256,128]{1,0:T(8,128)(2,1)}) custom-call(bf16[256,640]{1,0:T(8,128)(2,1)} %hid.1, f32[1,5120]{1,0:T(1,128)} %bitcast.4, s32[16]{0:T(128)} %seq_h.1, bf16[5120,384]{1,0:T(8,128)(2,1)} %wq.1, bf16[3,128]{1,0:T(4,128)(2,1)} %bitcast.5, bf16[5120,128]{1,0:T(8,128)(2,1)} %wk.1, ...), custom_call_target="tpu_custom_call" | custom-call | tf_op jit(solution)/shard_map/layer/pallas_call | solution.py:494
  72.2 1.8 %finish.1 = (bf16[256,640]{1,0:T(8,128)(2,1)}, bf16[256,128]{1,0:T(8,128)(2,1)}, bf16[256,128]{1,0:T(8,128)(2,1)}) custom-call(bf16[256,640]{1,0:T(8,128)(2,1)} %get-tuple-element.6.a, bf16[256,128]{1,0:T(8,128)(2,1)} %get-tuple-element.7.b, bf16[256,128]{1,0:T(8,128)(2,1)} %get-tuple-element.8.c), custom_call_target="tpu_custom_call" | custom-call | tf_op jit(solution)/shard_map/finish/pallas_call | solution.py:524

commit v5 on v4

--- a/solution.py
+++ b/solution.py
@@ -381,11 +381,11 @@
     loads[2].wait()
     queries()
     first_key()
+    plus(1)
+    minus(1)
     wait_for(None, 0, y, z, 1 - k)
     wait_for(None, 1, y, z, 1 - k)
     attend(y, z, True)
-    plus(1)
-    minus(1)
     cross(z)
     plus(2)
     visit(z - 1 >= 0, y, lo(1))
@@ -417,10 +417,26 @@
     visit(jnp.logical_and(y1, seen(lo(4))), zero, lo(4))
 
     gc = Gather(AT, H1, c_send, c_recv)
-    for h in range(NH):
-        o = ACC[h] / jnp.sum(L[h], axis=1, keepdims=True)
-        AT[:, pl.ds(pl.multiple_of(tp * H1 + h * HD, 128), HD)] = o.astype(BF)
-    gc.start()
+    def settle(c):
+        rows = pl.ds(c * (T // 4), T // 4)
+        for h in range(NH):
+            o = ACC[h, rows, :] / jnp.sum(L[h, rows, :], axis=1, keepdims=True)
+            AT[rows, pl.ds(pl.multiple_of(tp * H1 + h * HD, 128), HD)] = o.astype(BF)
+
+    settle(0)
+    settle(2)
+    gc.send(0, 0, right, LEFT)
+    gc.send(0, 2, left, RIGHT)
+    gc.send(0, 0, partner, PART)
+    settle(1)
+    settle(3)
+    gc.send(0, 1, right, LEFT)
+    gc.send(0, 3, left, RIGHT)
+    gc.send(0, 1, partner, PART)
+    gc.send(0, 2, right, LEFT)
+    gc.send(0, 0, left, RIGHT)
+    gc.send(0, 2, partner, PART)
+    gc.send(0, 3, partner, PART)
     loads[3].wait()
     OACC[...] = G[:, own_cols].astype(F32)
 

time: 74.3 us -> 74.2 us (level)
  no operation moved by 1% of the time
where the time goes in v5:
time: 74.2 us; the launch traced here: 73.8 us
  Pallas kernels  73 us (98%)
  between operations  0.8 us (1%)
    pallas_call x1, Pallas kernels, local(): pl.pallas_call(kernel, out_shape=(jax.ShapeDtypeStruct((T, D1), BF), jax....  71.2 us
    pallas_call x1, Pallas kernels, local(): pl.pallas_call(finish, out_shape=tuple((jax.ShapeDtypeStruct(m.shape, m.d...  1.82 us

profile of v5, /device:TPU:24, one launch (start us, length us, event | category | flops | bytes accessed | tf_op | source)
XLA Modules:
  0.0 73.8 jit_solution(9184684897924930172)
XLA Ops:
  0.6 71.2 %layer.1 = (bf16[256,640]{1,0:T(8,128)(2,1)}, bf16[256,128]{1,0:T(8,128)(2,1)}, bf16[256,128]{1,0:T(8,128)(2,1)}) custom-call(bf16[256,640]{1,0:T(8,128)(2,1)} %hid.1, f32[1,5120]{1,0:T(1,128)} %bitcast.4, s32[16]{0:T(128)} %seq_h.1, bf16[5120,384]{1,0:T(8,128)(2,1)} %wq.1, bf16[3,128]{1,0:T(4,128)(2,1)} %bitcast.5, bf16[5120,128]{1,0:T(8,128)(2,1)} %wk.1, ...), custom_call_target="tpu_custom_call" | custom-call | tf_op jit(solution)/shard_map/layer/pallas_call | solution.py:510
  71.8 1.8 %finish.1 = (bf16[256,640]{1,0:T(8,128)(2,1)}, bf16[256,128]{1,0:T(8,128)(2,1)}, bf16[256,128]{1,0:T(8,128)(2,1)}) custom-call(bf16[256,640]{1,0:T(8,128)(2,1)} %get-tuple-element.6.a, bf16[256,128]{1,0:T(8,128)(2,1)} %get-tuple-element.7.b, bf16[256,128]{1,0:T(8,128)(2,1)} %get-tuple-element.8.c), custom_call_target="tpu_custom_call" | custom-call | tf_op jit(solution)/shard_map/finish/pallas_call | solution.py:540
